TPU v7x, 32 devices: a whole 2x2x4 slice. The times are simulated.
32 devices in a mesh: dp: 4 (over y, x), expert: 8 (over z, core).
Axes of the slice: x: 2, y: 2, z: 4, core: 2. Of those that a mesh axis runs over, the one named last changes fastest.
Arguments:
- tokens: bfloat16 [8, 512, 4096], P('expert', 'dp'), may hold values from -6 to 6
- w_gate: bfloat16 [8, 4096, 896], P('expert'), may hold values from -0.09375 to 0.09375
- w_up: bfloat16 [8, 4096, 896], P('expert'), may hold values from -0.09375 to 0.09375
- w_down: bfloat16 [8, 896, 4096], P('expert'), may hold values from -0.1875 to 0.1875
- expert_ids: int32 [8, 512, 4], P('expert'), may hold values from 0 to 7, all different within a row
- gate_index: int32 [8, 512, 4], P('expert'), may hold values from 0 to 255
- gate_table: float32 [256], replicated, may hold values from 0.05 to 1
- spill: int32 [8, 512], P('expert'), may hold values from 0 to 3, as said below
Outputs:
- mixed: bfloat16 [8, 512, 4096], P('expert', 'dp')
Inputs may be any that keep to these rules, and one draw needn't show every extreme that they name: `spill`: A token is dispatched by a device of its own column. Of the 128 tokens of one device at most 32 are dispatched by any one other device, and in every draw some device hands exactly 32 to some peer.
All inputs are finite; a program needn't handle non-finite values.
Results may differ from a plain program's by a relative error of at most 0.0058.
Values may be sent and summed in bfloat16 or wider, within the bound.
A program may use at most 128 MiB of HBM per device.

v0:
```python
import functools
import jax
import jax.numpy as jnp
from jax import lax
from jax.experimental import pallas as pl
from jax.experimental.pallas import tpu as pltpu
from jax.sharding import PartitionSpec as P


def exchange_plan(tokens, w_gate, w_up, w_down, expert_ids, gate_index, gate_table, spill):
    dp_count = lax.axis_size("dp")
    expert_count = lax.axis_size("expert")
    local_experts = w_gate.shape[0]
    experts_all = local_experts * expert_count
    own_rows = tokens.shape[1]
    model_width = tokens.shape[2]
    column_tokens = spill.shape[1]
    top_count = expert_ids.shape[2]
    capacity = 3 * own_rows * top_count // (2 * experts_all)
    spill_room = own_rows // 4
    dp_index = lax.axis_index("dp")
    senders = spill[0]
    flat_ids = expert_ids[0].reshape(-1)
    level_count = gate_table.shape[0]
    matches = gate_index[0][:, :, None] == jnp.arange(level_count, dtype=jnp.int32)
    picked = jnp.sum(jnp.where(matches, gate_table, 0.0), axis=2)
    weight = picked / jnp.sum(picked, axis=1, keepdims=True)
    pair_sender = jnp.repeat(senders, top_count)
    is_mine = pair_sender == dp_index
    onehot = (
        (flat_ids[:, None] == jnp.arange(experts_all, dtype=jnp.int32)) & is_mine[:, None]
    ).astype(jnp.int32)
    slot_rank = jnp.sum((jnp.cumsum(onehot, axis=0) - onehot) * onehot, axis=1)
    is_kept = is_mine & (slot_rank < capacity)
    empty_slot = experts_all * capacity
    slot_index = jnp.where(is_kept, flat_ids * capacity + slot_rank, empty_slot)
    pair_token = jnp.arange(column_tokens * top_count, dtype=jnp.int32) // top_count
    zero_row = jnp.zeros((1, model_width), tokens.dtype)
    token_ids = jnp.arange(column_tokens, dtype=jnp.int32)
    home_dev = token_ids // own_rows
    local_token = token_ids - home_dev * own_rows
    is_moved = senders != home_dev
    route_key = home_dev * dp_count + senders
    route_hot = (route_key[:, None] == jnp.arange(dp_count * dp_count, dtype=jnp.int32)).astype(
        jnp.int32
    )
    spill_rank = jnp.sum((jnp.cumsum(route_hot, axis=0) - route_hot) * route_hot, axis=1)
    incoming = is_moved & (senders == dp_index)
    spill_slots = dp_count * spill_room
    outgoing = is_moved & (home_dev == dp_index)
    send_target = jnp.where(outgoing, senders * spill_room + spill_rank, spill_slots)
    send_source = (
        jnp.full((spill_slots,), own_rows, jnp.int32).at[send_target].set(local_token, mode="drop")
    )
    own_padded = jnp.concatenate([tokens[0], zero_row], axis=0)
    outgoing_rows = own_padded[send_source].reshape(dp_count, spill_room, model_width)
    arrived = lax.all_to_all(outgoing_rows, "dp", split_axis=0, concat_axis=0, tiled=True)
    source_rows = jnp.concatenate(
        [tokens[0], arrived.reshape(spill_slots, model_width), zero_row], axis=0
    )
    token_row = jnp.where(
        home_dev == dp_index,
        local_token,
        jnp.where(incoming, own_rows + home_dev * spill_room + spill_rank, own_rows + spill_slots),
    )
    dispatch_source = (
        jnp.full((empty_slot,), source_rows.shape[0] - 1, jnp.int32)
        .at[slot_index]
        .set(token_row[pair_token], mode="drop")
    )
    outbound = source_rows[dispatch_source].reshape(
        expert_count, local_experts, capacity, model_width
    )
    block = lax.all_to_all(outbound, "expert", split_axis=0, concat_axis=0, tiled=True)
    gate_part = jnp.einsum("aecd,edf->aecf", block, w_gate, preferred_element_type=jnp.float32)
    up_part = jnp.einsum("aecd,edf->aecf", block, w_up, preferred_element_type=jnp.float32)
    hidden = (jax.nn.silu(gate_part) * up_part).astype(jnp.bfloat16)
    expert_out = jnp.einsum(
        "aecf,efd->aecd", hidden, w_down, preferred_element_type=jnp.float32
    ).astype(jnp.bfloat16)
    returned = lax.all_to_all(expert_out, "expert", split_axis=0, concat_axis=0, tiled=True)
    results = jnp.concatenate([returned.reshape(empty_slot, model_width), zero_row], axis=0)
    slot_grid = jnp.concatenate(
        [
            slot_index.reshape(column_tokens, top_count),
            jnp.full((1, top_count), empty_slot, jnp.int32),
        ],
        axis=0,
    )
    kept_scale = jnp.where(is_kept.reshape(column_tokens, top_count), weight, 0.0)
    scale_grid = jnp.concatenate([kept_scale, jnp.zeros((1, top_count), jnp.float32)], axis=0)

    def combine(chosen):
        chosen_slots = slot_grid[chosen]
        chosen_scale = scale_grid[chosen]
        summed = jnp.zeros((chosen.shape[0], model_width), jnp.float32)
        for member in range(top_count):
            summed = summed + chosen_scale[:, member : member + 1] * results[
                chosen_slots[:, member]
            ].astype(jnp.float32)
        return summed

    own_ids = dp_index * own_rows + jnp.arange(own_rows, dtype=jnp.int32)
    own_part = combine(own_ids)
    arrived_target = jnp.where(incoming, home_dev * spill_room + spill_rank, spill_slots)
    arrived_ids = (
        jnp.full((spill_slots,), column_tokens, jnp.int32)
        .at[arrived_target]
        .set(token_ids, mode="drop")
    )
    arrived_part = combine(arrived_ids).reshape(dp_count, spill_room, model_width)
    returned_part = lax.all_to_all(
        arrived_part.astype(jnp.bfloat16), "dp", split_axis=0, concat_axis=0, tiled=True
    ).astype(arrived_part.dtype)
    back_rows = jnp.concatenate(
        [returned_part.reshape(spill_slots, model_width), jnp.zeros((1, model_width), jnp.float32)],
        axis=0,
    )
    back_pick = jnp.where(
        is_moved[own_ids], senders[own_ids] * spill_room + spill_rank[own_ids], spill_slots
    )
    mixed = own_part + back_rows[back_pick]
    return mixed.astype(jnp.bfloat16)[None]


CORES = 2
CHUNKS = 4
TILES = 8
LEAVE = 4
LAG = 2
MESH = pl.DeviceIdType.MESH


def token_scales(expert_ids, gate_index, gate_table, spill, own_rows, experts_all):
    top_count, column_tokens = expert_ids.shape[1:]
    capacity = 3 * own_rows * top_count // (2 * experts_all)
    first = pl.multiple_of(lax.axis_index("dp") * own_rows, own_rows)
    own = pl.ds(first, own_rows)
    experts = lax.broadcasted_iota(jnp.int32, (experts_all, column_tokens), 0)
    chosen = jnp.zeros((experts_all, column_tokens), jnp.float32)
    for k in range(top_count):
        chosen += jnp.where(expert_ids[0, k : k + 1, :] == experts, 1.0, 0.0)
    own_row = spill[:, own].astype(jnp.float32)
    own_senders = jnp.transpose(jnp.broadcast_to(own_row, (own_rows, own_rows)))[:, :1]
    shape = (own_rows, column_tokens)
    before = lax.broadcasted_iota(jnp.int32, shape, 1) < first + lax.broadcasted_iota(
        jnp.int32, shape, 0
    )
    earlier = before & (spill[...].astype(jnp.float32) == own_senders)
    rank = lax.dot_general(
        chosen.astype(jnp.bfloat16),
        jnp.where(earlier, 1.0, 0.0).astype(jnp.bfloat16),
        (((1,), (1,)), ((), ())),
        preferred_element_type=jnp.float32,
    )
    level_count = gate_table.shape[1]
    levels = lax.broadcasted_iota(jnp.int32, (level_count, own_rows), 0)
    table = jnp.transpose(jnp.broadcast_to(gate_table[...], (own_rows, level_count)))
    picked = [
        jnp.sum(
            jnp.where(gate_index[0, k : k + 1, own] == levels, table, 0.0), axis=0, keepdims=True
        )
        for k in range(top_count)
    ]
    norm = functools.reduce(jnp.add, picked)
    own_experts = lax.broadcasted_iota(jnp.int32, (experts_all, own_rows), 0)
    scale = jnp.zeros((experts_all, own_rows), jnp.float32)
    for k in range(top_count):
        scale += jnp.where(expert_ids[0, k : k + 1, own] == own_experts, picked[k] / norm, 0.0)
    return jnp.where(rank < capacity, scale, 0.0)


def line_kernel(
    chips, tok, w_gate, w_up, w_down, expert_ids, gate_index, gate_table, spill, out,
    x, w_in, w_out, scales, both, hid, part, near, from_left, from_right, going, total,
    own_sem, sc_s, sc_r, ag_right, ag_left, ag_r, ag_sib, sib_r, part_s, part_r, go_s, left_r, right_r,
):
    own_rows, width = tok.shape[1], tok.shape[2]
    hidden_units = w_gate.shape[2]
    piece = own_rows // CHUNKS
    tile = width // TILES
    count = chips * CORES
    me = lax.axis_index("expert")
    p = me // CORES
    q = lax.rem(me, CORES)
    sib = p * CORES + 1 - q
    right, left = me + CORES, me - CORES
    has_right, has_left = p < chips - 1, p > 0

    def send(src, dst, send_sem, recv_sem, device):
        return pltpu.make_async_remote_copy(
            src_ref=src, dst_ref=dst, send_sem=send_sem, recv_sem=recv_sem,
            device_id={"expert": device}, device_id_type=MESH,
        )

    def rows(c):
        return pl.ds(pl.multiple_of(c * piece, piece), piece)

    def gather_copy(s, c, sems, recv, device):
        block = x.at[CORES * s + q, rows(c)]
        return send(block, block, sems.at[s, c], recv.at[s, c], device)

    loads = [
        pltpu.make_async_copy(tok.at[0], x.at[me], own_sem.at[0]),
        pltpu.make_async_copy(w_gate.at[0], w_in.at[:, pl.ds(0, hidden_units)], own_sem.at[1]),
        pltpu.make_async_copy(w_up.at[0], w_in.at[:, pl.ds(hidden_units, hidden_units)], own_sem.at[2]),
        pltpu.make_async_copy(w_down.at[0], w_out, own_sem.at[3]),
    ]
    for load in loads:
        load.start()
    barrier = pltpu.get_barrier_semaphore()
    for step in range(1, count):
        pl.semaphore_signal(
            barrier, inc=1, device_id={"expert": lax.rem(me + step, count)}, device_id_type=MESH
        )
    pl.semaphore_wait(barrier, count - 1)
    loads[0].wait()

    def first_sends(c, carry):
        @pl.when(has_right)
        def _():
            gather_copy(p, c, ag_right, ag_r, right).start()

        @pl.when(has_left)
        def _():
            gather_copy(p, c, ag_left, ag_r, left).start()

        gather_copy(p, c, ag_sib, sib_r, sib).start()
        return carry

    lax.fori_loop(0, 1, first_sends, 0)
    scales[me] = token_scales(expert_ids, gate_index, gate_table, spill, tok.shape[1], count)
    mine = scales.at[me]
    for step in range(1, count):
        send(mine, mine, sc_s.at[step], sc_r.at[step], lax.rem(me + step, count)).start()
    lax.fori_loop(1, CHUNKS, first_sends, 0)
    for load in loads[1:]:
        load.wait()
    for step in range(1, count):
        send(
            mine, scales.at[lax.rem(me - step + count, count)], sc_s.at[step], sc_r.at[step], sib
        ).wait_recv()

    tall = CORES * own_rows
    in_tile = hidden_units
    out_tile = width // LEAVE
    per_leave = TILES // LEAVE

    def sib_wait(s):
        def one(c, carry):
            block = x.at[CORES * s + 1 - q, rows(c)]
            send(block, block, ag_sib.at[s, c], sib_r.at[s, c], sib).wait_recv()
            return carry

        lax.fori_loop(0, CHUNKS, one, 0)

    def expert(s):
        def enter(t, carry):
            cols = pl.ds(pl.multiple_of(t * in_tile, 128), in_tile)
            tokens = x[pl.ds(CORES * s, CORES)].reshape(tall, width)
            both[:, cols] = jnp.dot(tokens, w_in[:, cols], preferred_element_type=jnp.float32)
            return carry

        lax.fori_loop(0, 2 * hidden_units // in_tile, enter, 0)
        for core in range(CORES):
            part_rows = pl.ds(core * own_rows, own_rows)
            row = scales[CORES * s + core, pl.ds(me, 1), :]
            col = jnp.transpose(jnp.broadcast_to(row, (own_rows, own_rows)))[:, :1]
            gate = both[part_rows, pl.ds(0, hidden_units)]
            up = both[part_rows, pl.ds(hidden_units, hidden_units)]
            hid[part_rows, :] = (gate / (1.0 + jnp.exp(-gate)) * up * col).astype(hid.dtype)

        def pass_on(first):
            for c in range(per_leave):
                @pl.when((p == 0) & (s > p))
                def _():
                    onward(s, first + c, None, from_left, left_r, right)

                @pl.when((p == chips - 1) & (s < p))
                def _():
                    onward(s, first + c, None, from_right, right_r, left)

        def leave(t, carry):
            cols = pl.ds(pl.multiple_of(t * out_tile, 128), out_tile)
            made = jnp.dot(hid[...], w_out[:, cols], preferred_element_type=jnp.float32)
            made = made.astype(part.dtype).reshape(CORES, own_rows, out_tile)
            for c in range(per_leave):
                at = t * per_leave + c
                part[pl.ds(CORES * s, CORES), at] = made[:, :, c * tile : (c + 1) * tile]
                near_copy(s, at).start()

            @pl.when(t > 0)
            def _():
                pass_on((t - 1) * per_leave)

            return carry

        lax.fori_loop(0, LEAVE, leave, 0)
        pass_on(TILES - per_leave)

    def near_copy(s, c):
        return send(
            part.at[CORES * s + 1 - q, c], near.at[s, c], part_s.at[s, c], part_r.at[s, c], sib
        )

    def pair_sum(s, c):
        near_copy(s, c).wait_recv()
        return part[CORES * s + q, c].astype(jnp.float32) + near[s, c].astype(jnp.float32)

    def onward(s, c, up_sem, came, came_sem, device):
        if up_sem is None:
            going[s, c] = pair_sum(s, c).astype(going.dtype)
        else:
            block = going.at[s, c]
            send(block, came.at[s, c], go_s.at[s, c], up_sem.at[s, c], sib).wait_recv()
            going[s, c] = (pair_sum(s, c) + came[s, c].astype(jnp.float32)).astype(going.dtype)
        send(
            going.at[s, c], came.at[s, c], go_s.at[s, c], came_sem.at[s, c], device
        ).start()

    def slot(k, carry):
        for side in range(2):
            s = p - k if side == 0 else p + k
            valid = (s >= 0) if side == 0 else ((s < chips) & (k > 0))

            @pl.when(valid)
            def _():
                sib_wait(s)
                expert(s)

        def step(i, inner):
            to_right = i - LAG * (p - 1)

            @pl.when((p > 0) & (p < k) & (to_right >= 0) & (to_right < TILES))
            def _():
                onward(k, to_right, left_r, from_left, left_r, right)

            to_left = i - LAG * (chips - 2 - p)
            low = chips - 1 - k

            @pl.when((p < chips - 1) & (p > low) & (to_left >= 0) & (to_left < TILES))
            def _():
                onward(low, to_left, right_r, from_right, right_r, left)

            turn = TILES // CHUNKS
            gather = lax.rem(i, turn) == turn - 1
            g = i // turn

            before = p - k - 1

            @pl.when(gather & (g < CHUNKS) & (before >= 0))
            def _():
                gather_copy(before, g, ag_right, ag_r, sib).wait_recv()

                @pl.when(has_right)
                def _():
                    gather_copy(before, g, ag_right, ag_r, right).start()

                gather_copy(before, g, ag_sib, sib_r, sib).start()

            after = p + k + 1

            @pl.when(gather & (g < CHUNKS) & (after < chips))
            def _():
                gather_copy(after, g, ag_left, ag_r, sib).wait_recv()

                @pl.when(has_left)
                def _():
                    gather_copy(after, g, ag_left, ag_r, left).start()

                gather_copy(after, g, ag_sib, sib_r, sib).start()

            return inner

        lax.fori_loop(0, TILES + LAG * max(chips - 2, 0), step, 0)
        return carry

    lax.fori_loop(0, chips, slot, 0)

    def finish(c, carry):
        total[...] = pair_sum(p, c)
        for there, came, came_sem in (
            (has_left, from_left, left_r), (has_right, from_right, right_r)
        ):
            @pl.when(there)
            def _():
                block = came.at[p, c]
                send(block, block, go_s.at[p, c], came_sem.at[p, c], sib).wait_recv()
                total[...] += came[p, c].astype(jnp.float32)

        cols = pl.ds(pl.multiple_of(c * tile, 128), tile)
        out[0, :, cols] = total[...].astype(out.dtype)
        return carry

    lax.fori_loop(0, TILES, finish, 0)

    for step in range(1, count):
        send(mine, mine, sc_s.at[step], sc_r.at[step], sib).wait_send()

    def drain(s, carry):
        def gathered(c, inner):
            gather_copy(s, c, ag_sib, sib_r, sib).wait_send()

            @pl.when(has_right & (s <= p))
            def _():
                gather_copy(s, c, ag_right, ag_r, sib).wait_send()

            @pl.when(has_left & (s >= p))
            def _():
                gather_copy(s, c, ag_left, ag_r, sib).wait_send()

            return inner

        def summed(c, inner):
            near_copy(s, c).wait_send()

            @pl.when(s != p)
            def _():
                block = going.at[s, c]
                send(block, block, go_s.at[s, c], left_r.at[s, c], sib).wait_send()

            return inner

        lax.fori_loop(0, CHUNKS, gathered, 0)
        lax.fori_loop(0, TILES, summed, 0)
        return carry

    lax.fori_loop(0, chips, drain, 0)


def scratch_of(chips, own_rows, width, hidden_units, experts_all, dtype):
    count = chips * CORES
    tile = width // TILES
    halves = pltpu.VMEM((chips, TILES, own_rows, tile), dtype)
    dma = pltpu.SemaphoreType.DMA
    gather = dma((chips, CHUNKS))
    tiled = dma((chips, TILES))
    return [
        pltpu.VMEM((count, own_rows, width), dtype),
        pltpu.VMEM((width, 2 * hidden_units), dtype),
        pltpu.VMEM((hidden_units, width), dtype),
        pltpu.VMEM((count, experts_all, own_rows), jnp.float32),
        pltpu.VMEM((CORES * own_rows, 2 * hidden_units), jnp.float32),
        pltpu.VMEM((CORES * own_rows, hidden_units), dtype),
        pltpu.VMEM((count, TILES, own_rows, tile), dtype),
        halves,
        halves,
        halves,
        halves,
        pltpu.VMEM((own_rows, tile), jnp.float32),
        dma((4,)),
        dma((count,)),
        dma((count,)),
        gather, gather, gather, gather, gather,
        tiled, tiled, tiled, tiled, tiled,
    ]


def line_plan(tokens, w_gate, w_up, w_down, expert_ids, gate_index, gate_table, spill):
    experts_all = lax.axis_size("expert")
    own_rows, width = tokens.shape[1:]
    chips = experts_all // CORES
    anywhere = pl.BlockSpec(memory_space=pl.ANY)
    vmem = pl.BlockSpec(memory_space=pltpu.VMEM)
    return pl.pallas_call(
        functools.partial(line_kernel, chips),
        out_shape=jax.ShapeDtypeStruct(tokens.shape, tokens.dtype),
        in_specs=[anywhere] * 4 + [vmem] * 4,
        out_specs=vmem,
        scratch_shapes=scratch_of(
            chips, own_rows, width, w_gate.shape[2], experts_all, tokens.dtype
        ),
        compiler_params=pltpu.CompilerParams(
            collective_id=0, has_side_effects=True, vmem_limit_bytes=67043328
        ),
    )(
        tokens, w_gate, w_up, w_down,
        jnp.swapaxes(expert_ids, 1, 2), jnp.swapaxes(gate_index, 1, 2), gate_table[None], spill,
    )


def local(tokens, w_gate, w_up, w_down, *routing):
    own_rows, width = tokens.shape[1:]
    experts_all = lax.axis_size("expert")
    held = w_gate.size + w_up.size + w_down.size + 4 * experts_all * own_rows * width
    fits = held * tokens.dtype.itemsize <= 56 * 2**20
    if fits and w_gate.shape[0] == 1 and experts_all % CORES == 0:
        return line_plan(tokens, w_gate, w_up, w_down, *routing)
    return exchange_plan(tokens, w_gate, w_up, w_down, *routing)


def solution(mesh):
    in_specs = (
        P("expert", "dp", None),
        P("expert", None, None),
        P("expert", None, None),
        P("expert", None, None),
        P("expert", None, None),
        P("expert", None, None),
        P(),
        P("expert", None),
    )
    out_specs = P("expert", "dp", None)
    return jax.shard_map(local, mesh=mesh, in_specs=in_specs, out_specs=out_specs, check_vma=False)
```

profile of v0, /device:TPU:0, one launch (start us, length us, event | category | flops | bytes accessed | tf_op | source)
XLA Modules:
  0.0 124.6 jit_solution(13771073594467266375)
XLA Ops:
  0.0 122.3 %shard_map.82 = bf16[1,128,4096]{2,1,0:T(8,128)(2,1)} custom-call(bf16[1,128,4096]{2,1,0:T(8,128)(2,1)} %tok.1, bf16[1,4096,896]{2,1,0:T(8,128)(2,1)} %w_gate.1, bf16[1,4096,896]{2,1,0:T(8,128)(2,1)} %w_up.1, bf16[1,896,4096]{2,1,0:T(8,128)(2,1)} %w_down.1, s32[1,4,512]{2,1,0:T(4,128)} %bitcast.3, s32[1,4,512]{2,1,0:T(4,128)} %bitcast.4, f32[1,256]{1,0:T(1,128)} %bitcast.5, ...), custom_call_target="tpu_custom_call" | custom-call | tf_op jit(solution)/shard_map/pallas_call | solution.py:465
  122.3 2.3 %copy.10 = bf16[1,128,4096]{2,1,0:T(8,128)(2,1)} copy(bf16[1,128,4096]{2,1,0:T(8,128)(2,1)} %shard_map.82) | data formatting | bytes 2097152
where the time goes:
time: 125 us
  Pallas kernels  122 us (98%)
  local copies, waits for them, and re-layouts  2.29 us (2%)
    pallas_call x1, Pallas kernels, line_plan(): pl.pallas_call(functools.partial(line_kernel, chips), out_shape=jax.Shape...  122 us

commit v1 on v0

--- a/solution.py
+++ b/solution.py
@@ -124,10 +124,10 @@
 
 
 CORES = 2
-CHUNKS = 4
-TILES = 8
-LEAVE = 4
-LAG = 2
+HALVES = 2
+PIECES = 4
+LEAD = 2
+IN_TILES = 2
 MESH = pl.DeviceIdType.MESH
 
 
@@ -172,14 +172,17 @@
 
 def line_kernel(
     chips, tok, w_gate, w_up, w_down, expert_ids, gate_index, gate_table, spill, out,
-    x, w_in, w_out, scales, both, hid, part, near, from_left, from_right, going, total,
-    own_sem, sc_s, sc_r, ag_right, ag_left, ag_r, ag_sib, sib_r, part_s, part_r, go_s, left_r, right_r,
+    x, w_in, w_out, scales, cols_of, both, hid, part, near, from_left, from_right, going, total,
+    own_sem, sc_right, sc_left, sc_sib, sc_r, sc_sib_r,
+    ag_right, ag_left, ag_sib, ag_r, sib_r, part_s, part_r, go_s, left_r, right_r,
 ):
     own_rows, width = tok.shape[1], tok.shape[2]
     hidden_units = w_gate.shape[2]
-    piece = own_rows // CHUNKS
-    tile = width // TILES
+    half = own_rows // HALVES
+    piece = half // PIECES
+    tile = width // PIECES
     count = chips * CORES
+    slots = 2 * chips
     me = lax.axis_index("expert")
     p = me // CORES
     q = lax.rem(me, CORES)
@@ -193,12 +196,18 @@
             device_id={"expert": device}, device_id_type=MESH,
         )
 
-    def rows(c):
-        return pl.ds(pl.multiple_of(c * piece, piece), piece)
-
-    def gather_copy(s, c, sems, recv, device):
-        block = x.at[CORES * s + q, rows(c)]
-        return send(block, block, sems.at[s, c], recv.at[s, c], device)
+    def gather_copy(s, c, send_sem, recv_sem, device):
+        block = x.at[CORES * s + q, pl.ds(pl.multiple_of(c * piece, piece), piece)]
+        return send(block, block, send_sem.at[s], recv_sem.at[s, c], device)
+
+    def scale_copy(s, send_sem, recv_sem, device):
+        block = scales.at[CORES * s + q]
+        return send(block, block, send_sem.at[s], recv_sem.at[s], device)
+
+    sides = (
+        (p, has_right, right, ag_right, sc_right, from_left, left_r),
+        (chips - 1 - p, has_left, left, ag_left, sc_left, from_right, right_r),
+    )
 
     loads = [
         pltpu.make_async_copy(tok.at[0], x.at[me], own_sem.at[0]),
@@ -209,220 +218,214 @@
     for load in loads:
         load.start()
     barrier = pltpu.get_barrier_semaphore()
-    for step in range(1, count):
-        pl.semaphore_signal(
-            barrier, inc=1, device_id={"expert": lax.rem(me + step, count)}, device_id_type=MESH
-        )
-    pl.semaphore_wait(barrier, count - 1)
+
+    def greet(device):
+        pl.semaphore_signal(barrier, inc=1, device_id={"expert": device}, device_id_type=MESH)
+
+    greet(sib)
+    pl.when(has_right)(lambda: greet(right))
+    pl.when(has_left)(lambda: greet(left))
+    pl.semaphore_wait(barrier, 1 + has_right.astype(jnp.int32) + has_left.astype(jnp.int32))
     loads[0].wait()
 
     def first_sends(c, carry):
-        @pl.when(has_right)
-        def _():
-            gather_copy(p, c, ag_right, ag_r, right).start()
-
-        @pl.when(has_left)
-        def _():
-            gather_copy(p, c, ag_left, ag_r, left).start()
-
+        for _, there, device, ag, *_ in sides:
+            pl.when(there)(lambda: gather_copy(p, c, ag, ag_r, device).start())
+        return carry
+
+    def sib_sends(c, carry):
         gather_copy(p, c, ag_sib, sib_r, sib).start()
         return carry
 
-    lax.fori_loop(0, 1, first_sends, 0)
-    scales[me] = token_scales(expert_ids, gate_index, gate_table, spill, tok.shape[1], count)
-    mine = scales.at[me]
-    for step in range(1, count):
-        send(mine, mine, sc_s.at[step], sc_r.at[step], lax.rem(me + step, count)).start()
-    lax.fori_loop(1, CHUNKS, first_sends, 0)
-    for load in loads[1:]:
-        load.wait()
-    for step in range(1, count):
-        send(
-            mine, scales.at[lax.rem(me - step + count, count)], sc_s.at[step], sc_r.at[step], sib
-        ).wait_recv()
-
-    tall = CORES * own_rows
-    in_tile = hidden_units
-    out_tile = width // LEAVE
-    per_leave = TILES // LEAVE
-
-    def sib_wait(s):
-        def one(c, carry):
-            block = x.at[CORES * s + 1 - q, rows(c)]
-            send(block, block, ag_sib.at[s, c], sib_r.at[s, c], sib).wait_recv()
+    lax.fori_loop(0, PIECES, first_sends, 0)
+    lax.fori_loop(0, HALVES * PIECES, sib_sends, 0)
+    scales[me] = token_scales(expert_ids, gate_index, gate_table, spill, own_rows, count)
+    for _, there, device, _, sc, *_ in sides:
+        pl.when(there)(lambda: scale_copy(p, sc, sc_r, device).start())
+    scale_copy(p, sc_sib, sc_sib_r, sib).start()
+
+    tall = CORES * half
+    in_tile = 2 * hidden_units // IN_TILES
+
+    def block_rows(h):
+        return pl.ds(pl.multiple_of(h * half, half), half)
+
+    def enter(s, h):
+        @pl.when((s == p) & (h == 0))
+        def _():
+            loads[1].wait()
+            loads[2].wait()
+
+        def arrived(t, carry):
+            block = x.at[CORES * s + 1 - q, pl.ds(pl.multiple_of((h * PIECES + t) * piece, piece), piece)]
+            send(block, block, ag_sib.at[s], sib_r.at[s, h * PIECES + t], sib).wait_recv()
             return carry
 
-        lax.fori_loop(0, CHUNKS, one, 0)
-
-    def expert(s):
-        def enter(t, carry):
+        lax.fori_loop(0, PIECES, arrived, 0)
+
+        def one(t, carry):
             cols = pl.ds(pl.multiple_of(t * in_tile, 128), in_tile)
-            tokens = x[pl.ds(CORES * s, CORES)].reshape(tall, width)
+            tokens = x[pl.ds(CORES * s, CORES), block_rows(h)].reshape(tall, width)
             both[:, cols] = jnp.dot(tokens, w_in[:, cols], preferred_element_type=jnp.float32)
             return carry
 
-        lax.fori_loop(0, 2 * hidden_units // in_tile, enter, 0)
+        lax.fori_loop(0, IN_TILES, one, 0)
+
+    def near_copy(s, h, t):
+        return send(
+            part.at[CORES * s + 1 - q, h, t], near.at[s, h, t],
+            part_s.at[s], part_r.at[s, h * PIECES + t], sib,
+        )
+
+    def leave(s, h):
+        @pl.when((s == p) & (h == 0))
+        def _():
+            loads[3].wait()
+
+        @pl.when(h == 0)
+        def _():
+            block = scales.at[CORES * s + 1 - q]
+            send(block, block, sc_sib.at[s], sc_sib_r.at[s], sib).wait_recv()
+            for core in range(CORES):
+                row = scales[CORES * s + core, pl.ds(me, 1), :]
+                cols_of[s, core] = jnp.transpose(jnp.broadcast_to(row, (own_rows, own_rows)))
+
         for core in range(CORES):
-            part_rows = pl.ds(core * own_rows, own_rows)
-            row = scales[CORES * s + core, pl.ds(me, 1), :]
-            col = jnp.transpose(jnp.broadcast_to(row, (own_rows, own_rows)))[:, :1]
+            part_rows = pl.ds(core * half, half)
+            col = cols_of[s, core, block_rows(h), :][:, :1]
             gate = both[part_rows, pl.ds(0, hidden_units)]
             up = both[part_rows, pl.ds(hidden_units, hidden_units)]
             hid[part_rows, :] = (gate / (1.0 + jnp.exp(-gate)) * up * col).astype(hid.dtype)
 
-        def pass_on(first):
-            for c in range(per_leave):
-                @pl.when((p == 0) & (s > p))
+        def one(t, carry):
+            cols = pl.ds(pl.multiple_of(t * tile, 128), tile)
+            made = jnp.dot(hid[...], w_out[:, cols], preferred_element_type=jnp.float32)
+            part[pl.ds(CORES * s, CORES), h, t] = made.astype(part.dtype).reshape(CORES, half, tile)
+            near_copy(s, h, t).start()
+            return carry
+
+        lax.fori_loop(0, PIECES, one, 0)
+
+    def pair_sum(s, h, t):
+        return part[CORES * s + q, h, t].astype(jnp.float32) + near[s, h, t].astype(jnp.float32)
+
+    def came_wait(came, came_sem, s, h, t):
+        block = came.at[s, h, t]
+        send(block, block, go_s.at[s], came_sem.at[s, h * PIECES + t], sib).wait_recv()
+
+    def gathers(at, side, place, there, device, ag, sc, came, came_sem):
+        k, t = at // PIECES, lax.rem(at, PIECES)
+        h = (k > place).astype(jnp.int32)
+        origin = jnp.where(k > place, k - place - 1, place - k)
+        s = origin if side == 0 else chips - 1 - origin
+        active = (k > 0) & (k <= 2 * place + 1)
+        c = h * PIECES + t
+
+        @pl.when(active & (s != p))
+        def _():
+            gather_copy(s, c, ag, ag_r, sib).wait_recv()
+            gather_copy(s, c, ag_sib, sib_r, sib).start()
+
+            @pl.when(c == 0)
+            def _():
+                scale_copy(s, sc, sc_r, sib).wait_recv()
+                scale_copy(s, sc_sib, sc_sib_r, sib).start()
+                pl.when(there)(lambda: scale_copy(s, sc, sc_r, device).start())
+
+        pl.when(active & there)(lambda: gather_copy(s, c, ag, ag_r, device).start())
+
+    def sums(at, side, place, there, device, ag, sc, came, came_sem):
+        k, t = at // PIECES, lax.rem(at, PIECES)
+        i = k - (2 * place + 2)
+        n = chips - 1 - place
+        h = (i >= n).astype(jnp.int32)
+        target = place + 1 + jnp.where(i >= n, 2 * n - 1 - i, i)
+        s = target if side == 0 else chips - 1 - target
+
+        @pl.when((i >= 0) & (k < slots))
+        def _():
+            near_copy(s, h, t).wait_recv()
+
+            @pl.when(place == 0)
+            def _():
+                going[s, h, t] = pair_sum(s, h, t).astype(going.dtype)
+
+            @pl.when(place > 0)
+            def _():
+                came_wait(came, came_sem, s, h, t)
+                summed = pair_sum(s, h, t) + came[s, h, t].astype(jnp.float32)
+                going[s, h, t] = summed.astype(going.dtype)
+
+            send(
+                going.at[s, h, t], came.at[s, h, t],
+                go_s.at[s], came_sem.at[s, h * PIECES + t], device,
+            ).start()
+
+    def unit(k, second):
+        mirror = (p >= chips - p) == second
+        place = jnp.where(mirror, chips - 1 - p, p)
+        origin = jnp.where(k > place, k - place - 1, place - k)
+        own = k == 0
+        s = jnp.where(own, p, jnp.where(mirror, chips - 1 - origin, origin))
+        h = jnp.where(own, second.astype(jnp.int32), (k > place).astype(jnp.int32))
+        return own | (k <= 2 * place), s, h
+
+    def period(m, carry):
+        at = m + LEAD
+        for side, args in enumerate(sides):
+            @pl.when(at < slots * PIECES)
+            def _():
+                gathers(at, side, *args)
+
+        since = m - 1
+        k, phase = since // 4, lax.rem(since, 4)
+        active, s, h = unit(k, phase >= 2)
+        active &= (since >= 0) & (k < slots - 1)
+        pl.when(active & (lax.rem(phase, 2) == 0))(lambda: enter(s, h))
+        pl.when(active & (lax.rem(phase, 2) == 1))(lambda: leave(s, h))
+        for side, args in enumerate(sides):
+            sums(at, side, *args)
+
+        last = m - ((slots - HALVES) * PIECES + LEAD)
+        h_last, t_last = last // PIECES, lax.rem(last, PIECES)
+
+        @pl.when(last >= 0)
+        def _():
+            near_copy(p, h_last, t_last).wait_recv()
+            total[...] = pair_sum(p, h_last, t_last)
+            for there, came, came_sem in (
+                (has_left, from_left, left_r), (has_right, from_right, right_r)
+            ):
+                @pl.when(there)
                 def _():
-                    onward(s, first + c, None, from_left, left_r, right)
-
-                @pl.when((p == chips - 1) & (s < p))
-                def _():
-                    onward(s, first + c, None, from_right, right_r, left)
-
-        def leave(t, carry):
-            cols = pl.ds(pl.multiple_of(t * out_tile, 128), out_tile)
-            made = jnp.dot(hid[...], w_out[:, cols], preferred_element_type=jnp.float32)
-            made = made.astype(part.dtype).reshape(CORES, own_rows, out_tile)
-            for c in range(per_leave):
-                at = t * per_leave + c
-                part[pl.ds(CORES * s, CORES), at] = made[:, :, c * tile : (c + 1) * tile]
-                near_copy(s, at).start()
-
-            @pl.when(t > 0)
+                    came_wait(came, came_sem, p, h_last, t_last)
+                    total[...] += came[p, h_last, t_last].astype(jnp.float32)
+
+            cols = pl.ds(pl.multiple_of(t_last * tile, 128), tile)
+            out[0, block_rows(h_last), cols] = total[...].astype(out.dtype)
+
+        return carry
+
+    lax.fori_loop(0, slots * PIECES + LEAD, period, 0)
+
+    def drain(s, carry):
+        mine = x.at[CORES * s + q]
+        send(mine, mine, ag_sib.at[s], ag_r.at[s, 0], sib).wait_send()
+        scale_copy(s, sc_sib, sc_sib_r, sib).wait_send()
+        for there, ahead, ag, sc in ((has_right, s <= p, ag_right, sc_right), (has_left, s >= p, ag_left, sc_left)):
+            @pl.when(there & ahead)
             def _():
-                pass_on((t - 1) * per_leave)
-
-            return carry
-
-        lax.fori_loop(0, LEAVE, leave, 0)
-        pass_on(TILES - per_leave)
-
-    def near_copy(s, c):
-        return send(
-            part.at[CORES * s + 1 - q, c], near.at[s, c], part_s.at[s, c], part_r.at[s, c], sib
-        )
-
-    def pair_sum(s, c):
-        near_copy(s, c).wait_recv()
-        return part[CORES * s + q, c].astype(jnp.float32) + near[s, c].astype(jnp.float32)
-
-    def onward(s, c, up_sem, came, came_sem, device):
-        if up_sem is None:
-            going[s, c] = pair_sum(s, c).astype(going.dtype)
-        else:
-            block = going.at[s, c]
-            send(block, came.at[s, c], go_s.at[s, c], up_sem.at[s, c], sib).wait_recv()
-            going[s, c] = (pair_sum(s, c) + came[s, c].astype(jnp.float32)).astype(going.dtype)
-        send(
-            going.at[s, c], came.at[s, c], go_s.at[s, c], came_sem.at[s, c], device
-        ).start()
-
-    def slot(k, carry):
-        for side in range(2):
-            s = p - k if side == 0 else p + k
-            valid = (s >= 0) if side == 0 else ((s < chips) & (k > 0))
-
-            @pl.when(valid)
-            def _():
-                sib_wait(s)
-                expert(s)
-
-        def step(i, inner):
-            to_right = i - LAG * (p - 1)
-
-            @pl.when((p > 0) & (p < k) & (to_right >= 0) & (to_right < TILES))
-            def _():
-                onward(k, to_right, left_r, from_left, left_r, right)
-
-            to_left = i - LAG * (chips - 2 - p)
-            low = chips - 1 - k
-
-            @pl.when((p < chips - 1) & (p > low) & (to_left >= 0) & (to_left < TILES))
-            def _():
-                onward(low, to_left, right_r, from_right, right_r, left)
-
-            turn = TILES // CHUNKS
-            gather = lax.rem(i, turn) == turn - 1
-            g = i // turn
-
-            before = p - k - 1
-
-            @pl.when(gather & (g < CHUNKS) & (before >= 0))
-            def _():
-                gather_copy(before, g, ag_right, ag_r, sib).wait_recv()
-
-                @pl.when(has_right)
-                def _():
-                    gather_copy(before, g, ag_right, ag_r, right).start()
-
-                gather_copy(before, g, ag_sib, sib_r, sib).start()
-
-            after = p + k + 1
-
-            @pl.when(gather & (g < CHUNKS) & (after < chips))
-            def _():
-                gather_copy(after, g, ag_left, ag_r, sib).wait_recv()
-
-                @pl.when(has_left)
-                def _():
-                    gather_copy(after, g, ag_left, ag_r, left).start()
-
-                gather_copy(after, g, ag_sib, sib_r, sib).start()
-
-            return inner
-
-        lax.fori_loop(0, TILES + LAG * max(chips - 2, 0), step, 0)
-        return carry
-
-    lax.fori_loop(0, chips, slot, 0)
-
-    def finish(c, carry):
-        total[...] = pair_sum(p, c)
-        for there, came, came_sem in (
-            (has_left, from_left, left_r), (has_right, from_right, right_r)
-        ):
-            @pl.when(there)
-            def _():
-                block = came.at[p, c]
-                send(block, block, go_s.at[p, c], came_sem.at[p, c], sib).wait_recv()
-                total[...] += came[p, c].astype(jnp.float32)
-
-        cols = pl.ds(pl.multiple_of(c * tile, 128), tile)
-        out[0, :, cols] = total[...].astype(out.dtype)
-        return carry
-
-    lax.fori_loop(0, TILES, finish, 0)
-
-    for step in range(1, count):
-        send(mine, mine, sc_s.at[step], sc_r.at[step], sib).wait_send()
-
-    def drain(s, carry):
-        def gathered(c, inner):
-            gather_copy(s, c, ag_sib, sib_r, sib).wait_send()
-
-            @pl.when(has_right & (s <= p))
-            def _():
-                gather_copy(s, c, ag_right, ag_r, sib).wait_send()
-
-            @pl.when(has_left & (s >= p))
-            def _():
-                gather_copy(s, c, ag_left, ag_r, sib).wait_send()
-
-            return inner
-
-        def summed(c, inner):
-            near_copy(s, c).wait_send()
-
-            @pl.when(s != p)
-            def _():
-                block = going.at[s, c]
-                send(block, block, go_s.at[s, c], left_r.at[s, c], sib).wait_send()
-
-            return inner
-
-        lax.fori_loop(0, CHUNKS, gathered, 0)
-        lax.fori_loop(0, TILES, summed, 0)
+                send(mine, mine, ag.at[s], ag_r.at[s, 0], sib).wait_send()
+                scale_copy(s, sc, sc_r, sib).wait_send()
+
+        given = part.at[CORES * s + 1 - q]
+        send(given, given, part_s.at[s], ag_r.at[s, 0], sib).wait_send()
+
+        @pl.when(s != p)
+        def _():
+            block = going.at[s]
+            send(block, block, go_s.at[s], ag_r.at[s, 0], sib).wait_send()
+
         return carry
 
     lax.fori_loop(0, chips, drain, 0)
@@ -430,29 +433,27 @@
 
 def scratch_of(chips, own_rows, width, hidden_units, experts_all, dtype):
     count = chips * CORES
-    tile = width // TILES
-    halves = pltpu.VMEM((chips, TILES, own_rows, tile), dtype)
+    half = own_rows // HALVES
+    tile = width // PIECES
+    tiles = (HALVES, PIECES, half, tile)
+    sums = pltpu.VMEM((chips, *tiles), dtype)
     dma = pltpu.SemaphoreType.DMA
-    gather = dma((chips, CHUNKS))
-    tiled = dma((chips, TILES))
+    line = dma((chips,))
+    pieces = dma((chips, HALVES * PIECES))
     return [
         pltpu.VMEM((count, own_rows, width), dtype),
         pltpu.VMEM((width, 2 * hidden_units), dtype),
         pltpu.VMEM((hidden_units, width), dtype),
         pltpu.VMEM((count, experts_all, own_rows), jnp.float32),
-        pltpu.VMEM((CORES * own_rows, 2 * hidden_units), jnp.float32),
-        pltpu.VMEM((CORES * own_rows, hidden_units), dtype),
-        pltpu.VMEM((count, TILES, own_rows, tile), dtype),
-        halves,
-        halves,
-        halves,
-        halves,
-        pltpu.VMEM((own_rows, tile), jnp.float32),
+        pltpu.VMEM((chips, CORES, own_rows, own_rows), jnp.float32),
+        pltpu.VMEM((CORES * half, 2 * hidden_units), jnp.float32),
+        pltpu.VMEM((CORES * half, hidden_units), dtype),
+        pltpu.VMEM((count, *tiles), dtype),
+        sums, sums, sums, sums,
+        pltpu.VMEM((half, tile), jnp.float32),
         dma((4,)),
-        dma((count,)),
-        dma((count,)),
-        gather, gather, gather, gather, gather,
-        tiled, tiled, tiled, tiled, tiled,
+        line, line, line, line, line,
+        line, line, line, pieces, pieces, line, pieces, line, pieces, pieces,
     ]
 
 
@@ -484,7 +485,9 @@
     experts_all = lax.axis_size("expert")
     held = w_gate.size + w_up.size + w_down.size + 4 * experts_all * own_rows * width
     fits = held * tokens.dtype.itemsize <= 56 * 2**20
-    if fits and w_gate.shape[0] == 1 and experts_all % CORES == 0:
+    cut = own_rows % (HALVES * PIECES * 16) == 0 and width % (PIECES * 128) == 0
+    line = w_gate.shape[0] == 1 and experts_all % CORES == 0 and experts_all > CORES
+    if fits and cut and line:
         return line_plan(tokens, w_gate, w_up, w_down, *routing)
     return exchange_plan(tokens, w_gate, w_up, w_down, *routing)
 

time: 125 us -> 104 us (0.83)
  Pallas kernels: 122 us -> 101 us
    pallas_call x1, Pallas kernels: 122 us -> 101 us  [line_plan(): pl.pallas_call(functools.partial(line_kernel, chips), out_shape=jax.Shape...]
where the time goes in v1:
time: 104 us; the launch traced here: 103 us
  Pallas kernels  101 us (97%)
  local copies, waits for them, and re-layouts  2.29 us (2%)
    pallas_call x1, Pallas kernels, line_plan(): pl.pallas_call(functools.partial(line_kernel, chips), out_shape=jax.Shape...  101 us
    unnamed x1, local copies, waits for them, and re-layouts  2.29 us

profile of v1, /device:TPU:0, one launch (start us, length us, event | category | flops | bytes accessed | tf_op | source)
XLA Modules:
  0.0 103.3 jit_solution(7995279185617278031)
XLA Ops:
  0.0 101.0 %shard_map.82 = bf16[1,128,4096]{2,1,0:T(8,128)(2,1)} custom-call(bf16[1,128,4096]{2,1,0:T(8,128)(2,1)} %tok.1, bf16[1,4096,896]{2,1,0:T(8,128)(2,1)} %w_gate.1, bf16[1,4096,896]{2,1,0:T(8,128)(2,1)} %w_up.1, bf16[1,896,4096]{2,1,0:T(8,128)(2,1)} %w_down.1, s32[1,4,512]{2,1,0:T(4,128)} %bitcast.3, s32[1,4,512]{2,1,0:T(4,128)} %bitcast.4, f32[1,256]{1,0:T(1,128)} %bitcast.5, ...), custom_call_target="tpu_custom_call" | custom-call | tf_op jit(solution)/shard_map/pallas_call | solution.py:466
  101.0 2.3 %copy.10 = bf16[1,128,4096]{2,1,0:T(8,128)(2,1)} copy(bf16[1,128,4096]{2,1,0:T(8,128)(2,1)} %shard_map.82) | data formatting | bytes 2097152

commit v2 on v1

--- a/solution.py
+++ b/solution.py
@@ -126,8 +126,9 @@
 CORES = 2
 HALVES = 2
 PIECES = 4
-LEAD = 2
-IN_TILES = 2
+LEAD = PIECES // 2
+IN_TILES = 1
+OUT_TILES = 2
 MESH = pl.DeviceIdType.MESH
 
 
@@ -171,9 +172,9 @@
 
 
 def line_kernel(
-    chips, tok, w_gate, w_up, w_down, expert_ids, gate_index, gate_table, spill, out,
-    x, w_in, w_out, scales, cols_of, both, hid, part, near, from_left, from_right, going, total,
-    own_sem, sc_right, sc_left, sc_sib, sc_r, sc_sib_r,
+    chips, tok, w_gate, w_up, w_down, ids_in, index_in, table_in, spill_in, out,
+    expert_ids, gate_index, gate_table, spill, x, w_in, w_out, scales, cols_of, both, hid, part, near, from_left, from_right, going, total,
+    tok_sem, own_sem, sc_right, sc_left, sc_sib, sc_r, sc_sib_r,
     ag_right, ag_left, ag_sib, ag_r, sib_r, part_s, part_r, go_s, left_r, right_r,
 ):
     own_rows, width = tok.shape[1], tok.shape[2]
@@ -210,11 +211,21 @@
     )
 
     loads = [
-        pltpu.make_async_copy(tok.at[0], x.at[me], own_sem.at[0]),
+        pltpu.make_async_copy(ids_in, expert_ids, own_sem.at[0]),
+        pltpu.make_async_copy(index_in, gate_index, own_sem.at[4]),
+        pltpu.make_async_copy(table_in, gate_table, own_sem.at[5]),
+        pltpu.make_async_copy(spill_in, spill, own_sem.at[6]),
         pltpu.make_async_copy(w_gate.at[0], w_in.at[:, pl.ds(0, hidden_units)], own_sem.at[1]),
         pltpu.make_async_copy(w_up.at[0], w_in.at[:, pl.ds(hidden_units, hidden_units)], own_sem.at[2]),
         pltpu.make_async_copy(w_down.at[0], w_out, own_sem.at[3]),
     ]
+
+    def own_rows_load(c):
+        rows = pl.ds(pl.multiple_of(c * piece, piece), piece)
+        return pltpu.make_async_copy(tok.at[0, rows], x.at[me, rows], tok_sem.at[c])
+
+    for c in range(HALVES * PIECES):
+        own_rows_load(c).start()
     for load in loads:
         load.start()
     barrier = pltpu.get_barrier_semaphore()
@@ -226,25 +237,29 @@
     pl.when(has_right)(lambda: greet(right))
     pl.when(has_left)(lambda: greet(left))
     pl.semaphore_wait(barrier, 1 + has_right.astype(jnp.int32) + has_left.astype(jnp.int32))
-    loads[0].wait()
 
     def first_sends(c, carry):
+        own_rows_load(c).wait()
         for _, there, device, ag, *_ in sides:
             pl.when(there)(lambda: gather_copy(p, c, ag, ag_r, device).start())
         return carry
 
     def sib_sends(c, carry):
+        pl.when(c >= PIECES)(lambda: own_rows_load(c).wait())
         gather_copy(p, c, ag_sib, sib_r, sib).start()
         return carry
 
     lax.fori_loop(0, PIECES, first_sends, 0)
     lax.fori_loop(0, HALVES * PIECES, sib_sends, 0)
+    for load in loads[:-3]:
+        load.wait()
     scales[me] = token_scales(expert_ids, gate_index, gate_table, spill, own_rows, count)
     for _, there, device, _, sc, *_ in sides:
         pl.when(there)(lambda: scale_copy(p, sc, sc_r, device).start())
     scale_copy(p, sc_sib, sc_sib_r, sib).start()
 
     tall = CORES * half
+    wide = width // OUT_TILES
     in_tile = 2 * hidden_units // IN_TILES
 
     def block_rows(h):
@@ -253,8 +268,8 @@
     def enter(s, h):
         @pl.when((s == p) & (h == 0))
         def _():
-            loads[1].wait()
-            loads[2].wait()
+            loads[-3].wait()
+            loads[-2].wait()
 
         def arrived(t, carry):
             block = x.at[CORES * s + 1 - q, pl.ds(pl.multiple_of((h * PIECES + t) * piece, piece), piece)]
@@ -280,7 +295,7 @@
     def leave(s, h):
         @pl.when((s == p) & (h == 0))
         def _():
-            loads[3].wait()
+            loads[-1].wait()
 
         @pl.when(h == 0)
         def _():
@@ -297,14 +312,17 @@
             up = both[part_rows, pl.ds(hidden_units, hidden_units)]
             hid[part_rows, :] = (gate / (1.0 + jnp.exp(-gate)) * up * col).astype(hid.dtype)
 
-        def one(t, carry):
-            cols = pl.ds(pl.multiple_of(t * tile, 128), tile)
+        def one(g, carry):
+            cols = pl.ds(pl.multiple_of(g * wide, 128), wide)
             made = jnp.dot(hid[...], w_out[:, cols], preferred_element_type=jnp.float32)
-            part[pl.ds(CORES * s, CORES), h, t] = made.astype(part.dtype).reshape(CORES, half, tile)
-            near_copy(s, h, t).start()
+            made = made.astype(part.dtype).reshape(CORES, half, wide)
+            for j in range(PIECES // OUT_TILES):
+                t = g * (PIECES // OUT_TILES) + j
+                part[pl.ds(CORES * s, CORES), h, t] = made[:, :, j * tile : (j + 1) * tile]
+                near_copy(s, h, t).start()
             return carry
 
-        lax.fori_loop(0, PIECES, one, 0)
+        lax.fori_loop(0, OUT_TILES, one, 0)
 
     def pair_sum(s, h, t):
         return part[CORES * s + q, h, t].astype(jnp.float32) + near[s, h, t].astype(jnp.float32)
@@ -370,6 +388,20 @@
         h = jnp.where(own, second.astype(jnp.int32), (k > place).astype(jnp.int32))
         return own | (k <= 2 * place), s, h
 
+    def drain(s, carry):
+        mine = x.at[CORES * s + q]
+        send(mine, mine, ag_sib.at[s], ag_r.at[s, 0], sib).wait_send()
+        scale_copy(s, sc_sib, sc_sib_r, sib).wait_send()
+        for there, ahead, ag, sc in ((has_right, s <= p, ag_right, sc_right), (has_left, s >= p, ag_left, sc_left)):
+            @pl.when(there & ahead)
+            def _():
+                send(mine, mine, ag.at[s], ag_r.at[s, 0], sib).wait_send()
+                scale_copy(s, sc, sc_r, sib).wait_send()
+
+        given = part.at[CORES * s + 1 - q]
+        send(given, given, part_s.at[s], ag_r.at[s, 0], sib).wait_send()
+        return carry
+
     def period(m, carry):
         at = m + LEAD
         for side, args in enumerate(sides):
@@ -377,17 +409,22 @@
             def _():
                 gathers(at, side, *args)
 
-        since = m - 1
-        k, phase = since // 4, lax.rem(since, 4)
-        active, s, h = unit(k, phase >= 2)
+        since = m - (PIECES - 1 - LEAD)
+        k, phase = since // PIECES, lax.rem(since, PIECES)
+        active, s, h = unit(k, phase >= PIECES // 2)
+        step = lax.rem(phase, PIECES // 2)
         active &= (since >= 0) & (k < slots - 1)
-        pl.when(active & (lax.rem(phase, 2) == 0))(lambda: enter(s, h))
-        pl.when(active & (lax.rem(phase, 2) == 1))(lambda: leave(s, h))
+        pl.when(active & (step == 0))(lambda: enter(s, h))
+        pl.when(active & (step == 1))(lambda: leave(s, h))
         for side, args in enumerate(sides):
             sums(at, side, *args)
 
-        last = m - ((slots - HALVES) * PIECES + LEAD)
+        last = m - ((slots - HALVES) * PIECES + PIECES - LEAD)
         h_last, t_last = last // PIECES, lax.rem(last, PIECES)
+
+        @pl.when(last == PIECES)
+        def _():
+            lax.fori_loop(0, chips, drain, 0)
 
         @pl.when(last >= 0)
         def _():
@@ -406,21 +443,9 @@
 
         return carry
 
-    lax.fori_loop(0, slots * PIECES + LEAD, period, 0)
-
-    def drain(s, carry):
-        mine = x.at[CORES * s + q]
-        send(mine, mine, ag_sib.at[s], ag_r.at[s, 0], sib).wait_send()
-        scale_copy(s, sc_sib, sc_sib_r, sib).wait_send()
-        for there, ahead, ag, sc in ((has_right, s <= p, ag_right, sc_right), (has_left, s >= p, ag_left, sc_left)):
-            @pl.when(there & ahead)
-            def _():
-                send(mine, mine, ag.at[s], ag_r.at[s, 0], sib).wait_send()
-                scale_copy(s, sc, sc_r, sib).wait_send()
-
-        given = part.at[CORES * s + 1 - q]
-        send(given, given, part_s.at[s], ag_r.at[s, 0], sib).wait_send()
-
+    lax.fori_loop(0, slots * PIECES + PIECES - LEAD, period, 0)
+
+    def drain_sums(s, carry):
         @pl.when(s != p)
         def _():
             block = going.at[s]
@@ -428,10 +453,10 @@
 
         return carry
 
-    lax.fori_loop(0, chips, drain, 0)
-
-
-def scratch_of(chips, own_rows, width, hidden_units, experts_all, dtype):
+    lax.fori_loop(0, chips, drain_sums, 0)
+
+
+def scratch_of(chips, own_rows, width, hidden_units, experts_all, dtype, routing):
     count = chips * CORES
     half = own_rows // HALVES
     tile = width // PIECES
@@ -441,6 +466,7 @@
     line = dma((chips,))
     pieces = dma((chips, HALVES * PIECES))
     return [
+        *[pltpu.VMEM(value.shape, value.dtype) for value in routing],
         pltpu.VMEM((count, own_rows, width), dtype),
         pltpu.VMEM((width, 2 * hidden_units), dtype),
         pltpu.VMEM((hidden_units, width), dtype),
@@ -451,7 +477,8 @@
         pltpu.VMEM((count, *tiles), dtype),
         sums, sums, sums, sums,
         pltpu.VMEM((half, tile), jnp.float32),
-        dma((4,)),
+        dma((HALVES * PIECES,)),
+        dma((7,)),
         line, line, line, line, line,
         line, line, line, pieces, pieces, line, pieces, line, pieces, pieces,
     ]
@@ -463,20 +490,22 @@
     chips = experts_all // CORES
     anywhere = pl.BlockSpec(memory_space=pl.ANY)
     vmem = pl.BlockSpec(memory_space=pltpu.VMEM)
+    routing = (
+        jnp.swapaxes(expert_ids, 1, 2), jnp.swapaxes(gate_index, 1, 2), gate_table[None], spill
+    )
     return pl.pallas_call(
         functools.partial(line_kernel, chips),
-        out_shape=jax.ShapeDtypeStruct(tokens.shape, tokens.dtype),
-        in_specs=[anywhere] * 4 + [vmem] * 4,
+        out_shape=pltpu.VMEM(tokens.shape, tokens.dtype),
+        in_specs=[anywhere] * 8,
         out_specs=vmem,
         scratch_shapes=scratch_of(
-            chips, own_rows, width, w_gate.shape[2], experts_all, tokens.dtype
+            chips, own_rows, width, w_gate.shape[2], experts_all, tokens.dtype, routing
         ),
         compiler_params=pltpu.CompilerParams(
-            collective_id=0, has_side_effects=True, vmem_limit_bytes=67043328
+            collective_id=0, has_side_effects=True, vmem_limit_bytes=62914560
         ),
     )(
-        tokens, w_gate, w_up, w_down,
-        jnp.swapaxes(expert_ids, 1, 2), jnp.swapaxes(gate_index, 1, 2), gate_table[None], spill,
+        tokens, w_gate, w_up, w_down, *routing
     )
 
 
@@ -485,7 +514,7 @@
     experts_all = lax.axis_size("expert")
     held = w_gate.size + w_up.size + w_down.size + 4 * experts_all * own_rows * width
     fits = held * tokens.dtype.itemsize <= 56 * 2**20
-    cut = own_rows % (HALVES * PIECES * 16) == 0 and width % (PIECES * 128) == 0
+    cut = own_rows % (HALVES * PIECES * 8) == 0 and width % (PIECES * 128) == 0
     line = w_gate.shape[0] == 1 and experts_all % CORES == 0 and experts_all > CORES
     if fits and cut and line:
         return line_plan(tokens, w_gate, w_up, w_down, *routing)

time: 104 us -> 100 us (0.962)
  Pallas kernels: 101 us -> 98.9 us
  local copies, waits for them, and re-layouts: 2.29 us -> 0.97 us
    pallas_call x1, Pallas kernels: 101 us -> 98.9 us  [line_plan(): pl.pallas_call(functools.partial(line_kernel, chips), out_shape=pltpu.VME...]
    unnamed x1, local copies, waits for them, and re-layouts: 2.29 us -> 0.97 us
where the time goes in v2:
time: 100 us; the launch traced here: 99.9 us
  Pallas kernels  98.9 us (99%)
    pallas_call x1, Pallas kernels, line_plan(): pl.pallas_call(functools.partial(line_kernel, chips), out_shape=pltpu.VME...  98.9 us

profile of v2, /device:TPU:0, one launch (start us, length us, event | category | flops | bytes accessed | tf_op | source)
XLA Modules:
  0.0 99.9 jit_solution(3573640805116033266)
XLA Ops:
  0.0 98.9 %shard_map.82 = bf16[1,128,4096]{2,1,0:T(8,128)(2,1)S(1)} custom-call(bf16[1,128,4096]{2,1,0:T(8,128)(2,1)} %tok.1, bf16[1,4096,896]{2,1,0:T(8,128)(2,1)} %w_gate.1, bf16[1,4096,896]{2,1,0:T(8,128)(2,1)} %w_up.1, bf16[1,896,4096]{2,1,0:T(8,128)(2,1)} %w_down.1, s32[1,4,512]{2,1,0:T(4,128)} %bitcast.3, s32[1,4,512]{2,1,0:T(4,128)} %bitcast.4, ...), custom_call_target="tpu_custom_call" | custom-call | tf_op jit(solution)/shard_map/pallas_call | solution.py:496
  98.9 1.0 copy.10

commit v3 on v2

--- a/solution.py
+++ b/solution.py
@@ -174,8 +174,8 @@
 def line_kernel(
     chips, tok, w_gate, w_up, w_down, ids_in, index_in, table_in, spill_in, out,
     expert_ids, gate_index, gate_table, spill, x, w_in, w_out, scales, cols_of, both, hid, part, near, from_left, from_right, going, total,
-    tok_sem, own_sem, sc_right, sc_left, sc_sib, sc_r, sc_sib_r,
-    ag_right, ag_left, ag_sib, ag_r, sib_r, part_s, part_r, go_s, left_r, right_r,
+    tok_sem, own_sem, to_right, to_left, to_sib, sc_right, sc_left, sc_sib, sc_r, sc_sib_r,
+    ag_r, sib_r, part_r, sum_r,
 ):
     own_rows, width = tok.shape[1], tok.shape[2]
     hidden_units = w_gate.shape[2]
@@ -197,36 +197,43 @@
             device_id={"expert": device}, device_id_type=MESH,
         )
 
-    def gather_copy(s, c, send_sem, recv_sem, device):
-        block = x.at[CORES * s + q, pl.ds(pl.multiple_of(c * piece, piece), piece)]
-        return send(block, block, send_sem.at[s], recv_sem.at[s, c], device)
+    def rows_of(s, core, c):
+        return x.at[CORES * s + core, pl.ds(pl.multiple_of(c * piece, piece), piece)]
+
+    def gather_copy(s, c, send_sem, to, device):
+        block = rows_of(s, q, c)
+        return send(block, block, send_sem, ag_r.at[jnp.where(s > to, s - 1, s), c], device)
+
+    def sib_copy(s, c):
+        block = rows_of(s, q, c)
+        return send(block, block, to_sib, sib_r.at[s, c // PIECES], sib)
 
     def scale_copy(s, send_sem, recv_sem, device):
         block = scales.at[CORES * s + q]
-        return send(block, block, send_sem.at[s], recv_sem.at[s], device)
+        return send(block, block, send_sem, recv_sem.at[s], device)
 
     sides = (
-        (p, has_right, right, ag_right, sc_right, from_left, left_r),
-        (chips - 1 - p, has_left, left, ag_left, sc_left, from_right, right_r),
+        (p, has_right, right, p + 1, to_right, sc_right, from_left),
+        (chips - 1 - p, has_left, left, p - 1, to_left, sc_left, from_right),
     )
 
     loads = [
         pltpu.make_async_copy(ids_in, expert_ids, own_sem.at[0]),
-        pltpu.make_async_copy(index_in, gate_index, own_sem.at[4]),
-        pltpu.make_async_copy(table_in, gate_table, own_sem.at[5]),
-        pltpu.make_async_copy(spill_in, spill, own_sem.at[6]),
-        pltpu.make_async_copy(w_gate.at[0], w_in.at[:, pl.ds(0, hidden_units)], own_sem.at[1]),
-        pltpu.make_async_copy(w_up.at[0], w_in.at[:, pl.ds(hidden_units, hidden_units)], own_sem.at[2]),
-        pltpu.make_async_copy(w_down.at[0], w_out, own_sem.at[3]),
+        pltpu.make_async_copy(index_in, gate_index, own_sem.at[1]),
+        pltpu.make_async_copy(table_in, gate_table, own_sem.at[2]),
+        pltpu.make_async_copy(spill_in, spill, own_sem.at[3]),
+        pltpu.make_async_copy(w_gate.at[0], w_in.at[:, pl.ds(0, hidden_units)], own_sem.at[4]),
+        pltpu.make_async_copy(w_up.at[0], w_in.at[:, pl.ds(hidden_units, hidden_units)], own_sem.at[4]),
+        pltpu.make_async_copy(w_down.at[0], w_out, own_sem.at[5]),
     ]
 
-    def own_rows_load(c):
-        rows = pl.ds(pl.multiple_of(c * piece, piece), piece)
-        return pltpu.make_async_copy(tok.at[0, rows], x.at[me, rows], tok_sem.at[c])
-
-    for c in range(HALVES * PIECES):
-        own_rows_load(c).start()
-    for load in loads:
+    def own_rows_load(h):
+        rows = pl.ds(h * half, half)
+        return pltpu.make_async_copy(tok.at[0, rows], x.at[me, rows], tok_sem.at[h])
+
+    for h in range(HALVES):
+        own_rows_load(h).start()
+    for load in loads[:-3]:
         load.start()
     barrier = pltpu.get_barrier_semaphore()
 
@@ -239,22 +246,24 @@
     pl.semaphore_wait(barrier, 1 + has_right.astype(jnp.int32) + has_left.astype(jnp.int32))
 
     def first_sends(c, carry):
-        own_rows_load(c).wait()
-        for _, there, device, ag, *_ in sides:
-            pl.when(there)(lambda: gather_copy(p, c, ag, ag_r, device).start())
+        for _, there, device, to, gone, *_ in sides:
+            pl.when(there)(lambda: gather_copy(p, c, gone, to, device).start())
         return carry
 
     def sib_sends(c, carry):
-        pl.when(c >= PIECES)(lambda: own_rows_load(c).wait())
-        gather_copy(p, c, ag_sib, sib_r, sib).start()
+        sib_copy(p, c).start()
         return carry
 
+    own_rows_load(0).wait()
     lax.fori_loop(0, PIECES, first_sends, 0)
+    own_rows_load(1).wait()
     lax.fori_loop(0, HALVES * PIECES, sib_sends, 0)
+    for load in loads[-3:]:
+        load.start()
     for load in loads[:-3]:
         load.wait()
     scales[me] = token_scales(expert_ids, gate_index, gate_table, spill, own_rows, count)
-    for _, there, device, _, sc, *_ in sides:
+    for _, there, device, _, _, sc, _ in sides:
         pl.when(there)(lambda: scale_copy(p, sc, sc_r, device).start())
     scale_copy(p, sc_sib, sc_sib_r, sib).start()
 
@@ -268,15 +277,10 @@
     def enter(s, h):
         @pl.when((s == p) & (h == 0))
         def _():
-            loads[-3].wait()
-            loads[-2].wait()
-
-        def arrived(t, carry):
-            block = x.at[CORES * s + 1 - q, pl.ds(pl.multiple_of((h * PIECES + t) * piece, piece), piece)]
-            send(block, block, ag_sib.at[s], sib_r.at[s, h * PIECES + t], sib).wait_recv()
-            return carry
-
-        lax.fori_loop(0, PIECES, arrived, 0)
+            pltpu.make_async_copy(w_in, w_in, own_sem.at[4]).wait()
+
+        block = x.at[CORES * s + 1 - q, block_rows(h)]
+        send(block, block, to_sib, sib_r.at[s, h], sib).wait_recv()
 
         def one(t, carry):
             cols = pl.ds(pl.multiple_of(t * in_tile, 128), in_tile)
@@ -289,8 +293,12 @@
     def near_copy(s, h, t):
         return send(
             part.at[CORES * s + 1 - q, h, t], near.at[s, h, t],
-            part_s.at[s], part_r.at[s, h * PIECES + t], sib,
+            to_sib, part_r.at[s, h], sib,
         )
+
+    def near_wait(s, h):
+        block = near.at[s, h]
+        send(block, block, to_sib, part_r.at[s, h], sib).wait_recv()
 
     def leave(s, h):
         @pl.when((s == p) & (h == 0))
@@ -300,7 +308,7 @@
         @pl.when(h == 0)
         def _():
             block = scales.at[CORES * s + 1 - q]
-            send(block, block, sc_sib.at[s], sc_sib_r.at[s], sib).wait_recv()
+            send(block, block, sc_sib, sc_sib_r.at[s], sib).wait_recv()
             for core in range(CORES):
                 row = scales[CORES * s + core, pl.ds(me, 1), :]
                 cols_of[s, core] = jnp.transpose(jnp.broadcast_to(row, (own_rows, own_rows)))
@@ -327,11 +335,14 @@
     def pair_sum(s, h, t):
         return part[CORES * s + q, h, t].astype(jnp.float32) + near[s, h, t].astype(jnp.float32)
 
-    def came_wait(came, came_sem, s, h, t):
+    def sum_sem(side, s, h, t):
+        return sum_r.at[s + 1 if side == 0 else s, h * PIECES + t]
+
+    def came_wait(side, came, s, h, t):
         block = came.at[s, h, t]
-        send(block, block, go_s.at[s], came_sem.at[s, h * PIECES + t], sib).wait_recv()
-
-    def gathers(at, side, place, there, device, ag, sc, came, came_sem):
+        send(block, block, to_sib, sum_sem(side, s, h, t), sib).wait_recv()
+
+    def gathers(at, side, place, there, device, to, gone, sc, came):
         k, t = at // PIECES, lax.rem(at, PIECES)
         h = (k > place).astype(jnp.int32)
         origin = jnp.where(k > place, k - place - 1, place - k)
@@ -341,8 +352,8 @@
 
         @pl.when(active & (s != p))
         def _():
-            gather_copy(s, c, ag, ag_r, sib).wait_recv()
-            gather_copy(s, c, ag_sib, sib_r, sib).start()
+            gather_copy(s, c, gone, p, sib).wait_recv()
+            sib_copy(s, c).start()
 
             @pl.when(c == 0)
             def _():
@@ -350,9 +361,9 @@
                 scale_copy(s, sc_sib, sc_sib_r, sib).start()
                 pl.when(there)(lambda: scale_copy(s, sc, sc_r, device).start())
 
-        pl.when(active & there)(lambda: gather_copy(s, c, ag, ag_r, device).start())
-
-    def sums(at, side, place, there, device, ag, sc, came, came_sem):
+        pl.when(active & there)(lambda: gather_copy(s, c, gone, to, device).start())
+
+    def sums(at, side, place, there, device, to, gone, sc, came):
         k, t = at // PIECES, lax.rem(at, PIECES)
         i = k - (2 * place + 2)
         n = chips - 1 - place
@@ -362,7 +373,7 @@
 
         @pl.when((i >= 0) & (k < slots))
         def _():
-            near_copy(s, h, t).wait_recv()
+            pl.when(t == 0)(lambda: near_wait(s, h))
 
             @pl.when(place == 0)
             def _():
@@ -370,13 +381,12 @@
 
             @pl.when(place > 0)
             def _():
-                came_wait(came, came_sem, s, h, t)
+                came_wait(side, came, s, h, t)
                 summed = pair_sum(s, h, t) + came[s, h, t].astype(jnp.float32)
                 going[s, h, t] = summed.astype(going.dtype)
 
             send(
-                going.at[s, h, t], came.at[s, h, t],
-                go_s.at[s], came_sem.at[s, h * PIECES + t], device,
+                going.at[s, h, t], came.at[s, h, t], gone, sum_sem(side, s, h, t), device
             ).start()
 
     def unit(k, second):
@@ -387,20 +397,6 @@
         s = jnp.where(own, p, jnp.where(mirror, chips - 1 - origin, origin))
         h = jnp.where(own, second.astype(jnp.int32), (k > place).astype(jnp.int32))
         return own | (k <= 2 * place), s, h
-
-    def drain(s, carry):
-        mine = x.at[CORES * s + q]
-        send(mine, mine, ag_sib.at[s], ag_r.at[s, 0], sib).wait_send()
-        scale_copy(s, sc_sib, sc_sib_r, sib).wait_send()
-        for there, ahead, ag, sc in ((has_right, s <= p, ag_right, sc_right), (has_left, s >= p, ag_left, sc_left)):
-            @pl.when(there & ahead)
-            def _():
-                send(mine, mine, ag.at[s], ag_r.at[s, 0], sib).wait_send()
-                scale_copy(s, sc, sc_r, sib).wait_send()
-
-        given = part.at[CORES * s + 1 - q]
-        send(given, given, part_s.at[s], ag_r.at[s, 0], sib).wait_send()
-        return carry
 
     def period(m, carry):
         at = m + LEAD
@@ -422,20 +418,14 @@
         last = m - ((slots - HALVES) * PIECES + PIECES - LEAD)
         h_last, t_last = last // PIECES, lax.rem(last, PIECES)
 
-        @pl.when(last == PIECES)
-        def _():
-            lax.fori_loop(0, chips, drain, 0)
-
         @pl.when(last >= 0)
         def _():
-            near_copy(p, h_last, t_last).wait_recv()
+            pl.when(t_last == 0)(lambda: near_wait(p, h_last))
             total[...] = pair_sum(p, h_last, t_last)
-            for there, came, came_sem in (
-                (has_left, from_left, left_r), (has_right, from_right, right_r)
-            ):
-                @pl.when(there)
+            for side, (place, *_, came) in enumerate(sides):
+                @pl.when(place > 0)
                 def _():
-                    came_wait(came, came_sem, p, h_last, t_last)
+                    came_wait(side, came, p, h_last, t_last)
                     total[...] += came[p, h_last, t_last].astype(jnp.float32)
 
             cols = pl.ds(pl.multiple_of(t_last * tile, 128), tile)
@@ -445,15 +435,21 @@
 
     lax.fori_loop(0, slots * PIECES + PIECES - LEAD, period, 0)
 
-    def drain_sums(s, carry):
-        @pl.when(s != p)
-        def _():
-            block = going.at[s]
-            send(block, block, go_s.at[s], ag_r.at[s, 0], sib).wait_send()
-
-        return carry
-
-    lax.fori_loop(0, chips, drain_sums, 0)
+    for place, there, _, _, gone, sc, _ in sides:
+        @pl.when(there)
+        def _():
+            block = x.at[pl.ds(0, chips)]
+            send(block, block, gone, sib_r.at[0, 0], sib).wait_send()
+
+        for k in range(chips):
+            @pl.when(there & (place == k))
+            def _():
+                block = scales.at[pl.ds(0, k + 1)]
+                send(block, block, sc, sib_r.at[0, 0], sib).wait_send()
+
+    block = scales.at[pl.ds(0, chips)]
+    send(block, block, sc_sib, sib_r.at[0, 0], sib).wait_send()
+    send(x, x, to_sib, sib_r.at[0, 0], sib).wait_send()
 
 
 def scratch_of(chips, own_rows, width, hidden_units, experts_all, dtype, routing):
@@ -463,8 +459,6 @@
     tiles = (HALVES, PIECES, half, tile)
     sums = pltpu.VMEM((chips, *tiles), dtype)
     dma = pltpu.SemaphoreType.DMA
-    line = dma((chips,))
-    pieces = dma((chips, HALVES * PIECES))
     return [
         *[pltpu.VMEM(value.shape, value.dtype) for value in routing],
         pltpu.VMEM((count, own_rows, width), dtype),
@@ -477,10 +471,15 @@
         pltpu.VMEM((count, *tiles), dtype),
         sums, sums, sums, sums,
         pltpu.VMEM((half, tile), jnp.float32),
-        dma((HALVES * PIECES,)),
-        dma((7,)),
-        line, line, line, line, line,
-        line, line, line, pieces, pieces, line, pieces, line, pieces, pieces,
+        dma((HALVES,)),
+        dma((6,)),
+        dma, dma, dma, dma, dma, dma,
+        dma((chips,)),
+        dma((chips,)),
+        dma((chips - 1, HALVES * PIECES)),
+        dma((chips, HALVES)),
+        dma((chips, HALVES)),
+        dma((chips + 1, HALVES * PIECES)),
     ]
 
 

time: 100 us -> 99 us (0.990)
  Pallas kernels: 98.9 us -> 97.8 us
    pallas_call x1, Pallas kernels: 98.9 us -> 97.8 us  [line_plan(): pl.pallas_call(functools.partial(line_kernel, chips), out_shape=pltpu.VME...]
where the time goes in v3:
time: 99 us; the launch traced here: 98.8 us
  Pallas kernels  97.8 us (99%)
    pallas_call x1, Pallas kernels, line_plan(): pl.pallas_call(functools.partial(line_kernel, chips), out_shape=pltpu.VME...  97.8 us

profile of v3, /device:TPU:0, one launch (start us, length us, event | category | flops | bytes accessed | tf_op | source)
XLA Modules:
  0.0 98.8 jit_solution(3407028234640756508)
XLA Ops:
  0.0 97.8 %shard_map.82 = bf16[1,128,4096]{2,1,0:T(8,128)(2,1)S(1)} custom-call(bf16[1,128,4096]{2,1,0:T(8,128)(2,1)} %tok.1, bf16[1,4096,896]{2,1,0:T(8,128)(2,1)} %w_gate.1, bf16[1,4096,896]{2,1,0:T(8,128)(2,1)} %w_up.1, bf16[1,896,4096]{2,1,0:T(8,128)(2,1)} %w_down.1, s32[1,4,512]{2,1,0:T(4,128)} %bitcast.3, s32[1,4,512]{2,1,0:T(4,128)} %bitcast.4, ...), custom_call_target="tpu_custom_call" | custom-call | tf_op jit(solution)/shard_map/pallas_call | solution.py:495
  97.8 1.0 copy.10

commit v4 on v3

--- a/solution.py
+++ b/solution.py
@@ -126,6 +126,7 @@
 CORES = 2
 HALVES = 2
 PIECES = 4
+PAIR = 2
 LEAD = PIECES // 2
 IN_TILES = 1
 OUT_TILES = 2
@@ -173,7 +174,7 @@
 
 def line_kernel(
     chips, tok, w_gate, w_up, w_down, ids_in, index_in, table_in, spill_in, out,
-    expert_ids, gate_index, gate_table, spill, x, w_in, w_out, scales, cols_of, both, hid, part, near, from_left, from_right, going, total,
+    expert_ids, gate_index, gate_table, spill, x, w_in, w_out, scales, cols_of, both, hid, part, near, from_left, from_right, going,
     tok_sem, own_sem, to_right, to_left, to_sib, sc_right, sc_left, sc_sib, sc_r, sc_sib_r,
     ag_r, sib_r, part_r, sum_r,
 ):
@@ -202,7 +203,12 @@
 
     def gather_copy(s, c, send_sem, to, device):
         block = rows_of(s, q, c)
-        return send(block, block, send_sem, ag_r.at[jnp.where(s > to, s - 1, s), c], device)
+        return send(block, block, send_sem, ag_r.at[jnp.where(s > to, s - 1, s), c // PAIR], device)
+
+    def pair_wait(s, pair):
+        rows = pl.ds(pl.multiple_of(pair * PAIR * piece, PAIR * piece), PAIR * piece)
+        block = x.at[CORES * s + q, rows]
+        send(block, block, to_sib, ag_r.at[jnp.where(s > p, s - 1, s), pair], sib).wait_recv()
 
     def sib_copy(s, c):
         block = rows_of(s, q, c)
@@ -217,6 +223,14 @@
         (chips - 1 - p, has_left, left, p - 1, to_left, sc_left, from_right),
     )
 
+    barrier = pltpu.get_barrier_semaphore()
+
+    def greet(device):
+        pl.semaphore_signal(barrier, inc=1, device_id={"expert": device}, device_id_type=MESH)
+
+    greet(sib)
+    pl.when(has_right)(lambda: greet(right))
+    pl.when(has_left)(lambda: greet(left))
     loads = [
         pltpu.make_async_copy(ids_in, expert_ids, own_sem.at[0]),
         pltpu.make_async_copy(index_in, gate_index, own_sem.at[1]),
@@ -235,14 +249,6 @@
         own_rows_load(h).start()
     for load in loads[:-3]:
         load.start()
-    barrier = pltpu.get_barrier_semaphore()
-
-    def greet(device):
-        pl.semaphore_signal(barrier, inc=1, device_id={"expert": device}, device_id_type=MESH)
-
-    greet(sib)
-    pl.when(has_right)(lambda: greet(right))
-    pl.when(has_left)(lambda: greet(left))
     pl.semaphore_wait(barrier, 1 + has_right.astype(jnp.int32) + has_left.astype(jnp.int32))
 
     def first_sends(c, carry):
@@ -336,11 +342,13 @@
         return part[CORES * s + q, h, t].astype(jnp.float32) + near[s, h, t].astype(jnp.float32)
 
     def sum_sem(side, s, h, t):
-        return sum_r.at[s + 1 if side == 0 else s, h * PIECES + t]
+        return sum_r.at[s + 1 if side == 0 else s, h * (PIECES // PAIR) + t // PAIR]
 
     def came_wait(side, came, s, h, t):
-        block = came.at[s, h, t]
-        send(block, block, to_sib, sum_sem(side, s, h, t), sib).wait_recv()
+        @pl.when(lax.rem(t, PAIR) == 0)
+        def _():
+            block = came.at[s, h, pl.ds(t // PAIR * PAIR, PAIR)]
+            send(block, block, to_sib, sum_sem(side, s, h, t), sib).wait_recv()
 
     def gathers(at, side, place, there, device, to, gone, sc, came):
         k, t = at // PIECES, lax.rem(at, PIECES)
@@ -352,7 +360,7 @@
 
         @pl.when(active & (s != p))
         def _():
-            gather_copy(s, c, gone, p, sib).wait_recv()
+            pl.when(lax.rem(t, PAIR) == 0)(lambda: pair_wait(s, c // PAIR))
             sib_copy(s, c).start()
 
             @pl.when(c == 0)
@@ -397,6 +405,18 @@
         s = jnp.where(own, p, jnp.where(mirror, chips - 1 - origin, origin))
         h = jnp.where(own, second.astype(jnp.int32), (k > place).astype(jnp.int32))
         return own | (k <= 2 * place), s, h
+
+    def drain():
+        for place, there, _, _, _, sc, _ in sides:
+            for k in range(chips):
+                @pl.when(there & (place == k))
+                def _():
+                    block = scales.at[pl.ds(0, k + 1)]
+                    send(block, block, sc, sib_r.at[0, 0], sib).wait_send()
+
+        block = scales.at[pl.ds(0, chips)]
+        send(block, block, sc_sib, sib_r.at[0, 0], sib).wait_send()
+        send(x, x, to_sib, sib_r.at[0, 0], sib).wait_send()
 
     def period(m, carry):
         at = m + LEAD
@@ -418,38 +438,34 @@
         last = m - ((slots - HALVES) * PIECES + PIECES - LEAD)
         h_last, t_last = last // PIECES, lax.rem(last, PIECES)
 
+        pl.when(last == PIECES)(drain)
+
         @pl.when(last >= 0)
         def _():
             pl.when(t_last == 0)(lambda: near_wait(p, h_last))
-            total[...] = pair_sum(p, h_last, t_last)
+            cols = pl.ds(pl.multiple_of(t_last * tile, 128), tile)
             for side, (place, *_, came) in enumerate(sides):
-                @pl.when(place > 0)
-                def _():
-                    came_wait(side, came, p, h_last, t_last)
-                    total[...] += came[p, h_last, t_last].astype(jnp.float32)
-
-            cols = pl.ds(pl.multiple_of(t_last * tile, 128), tile)
-            out[0, block_rows(h_last), cols] = total[...].astype(out.dtype)
+                pl.when(place > 0)(lambda: came_wait(side, came, p, h_last, t_last))
+
+            def finish(*arrived):
+                total = pair_sum(p, h_last, t_last)
+                for came in arrived:
+                    total += came[p, h_last, t_last].astype(jnp.float32)
+                out[0, block_rows(h_last), cols] = total.astype(out.dtype)
+
+            pl.when(has_left & has_right)(lambda: finish(from_left, from_right))
+            pl.when(jnp.logical_not(has_left))(lambda: finish(from_right))
+            pl.when(jnp.logical_not(has_right))(lambda: finish(from_left))
 
         return carry
 
     lax.fori_loop(0, slots * PIECES + PIECES - LEAD, period, 0)
 
-    for place, there, _, _, gone, sc, _ in sides:
+    for _, there, _, _, gone, *_ in sides:
         @pl.when(there)
         def _():
             block = x.at[pl.ds(0, chips)]
             send(block, block, gone, sib_r.at[0, 0], sib).wait_send()
-
-        for k in range(chips):
-            @pl.when(there & (place == k))
-            def _():
-                block = scales.at[pl.ds(0, k + 1)]
-                send(block, block, sc, sib_r.at[0, 0], sib).wait_send()
-
-    block = scales.at[pl.ds(0, chips)]
-    send(block, block, sc_sib, sib_r.at[0, 0], sib).wait_send()
-    send(x, x, to_sib, sib_r.at[0, 0], sib).wait_send()
 
 
 def scratch_of(chips, own_rows, width, hidden_units, experts_all, dtype, routing):
@@ -470,16 +486,15 @@
         pltpu.VMEM((CORES * half, hidden_units), dtype),
         pltpu.VMEM((count, *tiles), dtype),
         sums, sums, sums, sums,
-        pltpu.VMEM((half, tile), jnp.float32),
         dma((HALVES,)),
         dma((6,)),
         dma, dma, dma, dma, dma, dma,
         dma((chips,)),
         dma((chips,)),
-        dma((chips - 1, HALVES * PIECES)),
+        dma((chips - 1, HALVES * PIECES // PAIR)),
         dma((chips, HALVES)),
         dma((chips, HALVES)),
-        dma((chips + 1, HALVES * PIECES)),
+        dma((chips + 1, HALVES * PIECES // PAIR)),
     ]
 
 

time: 99 us -> 98.9 us (level)
  no operation moved by 1% of the time
where the time goes in v4:
time: 98.9 us; the launch traced here: 98.7 us
  Pallas kernels  97.7 us (99%)
    pallas_call x1, Pallas kernels, line_plan(): pl.pallas_call(functools.partial(line_kernel, chips), out_shape=pltpu.VME...  97.7 us

profile of v4, /device:TPU:0, one launch (start us, length us, event | category | flops | bytes accessed | tf_op | source)
XLA Modules:
  0.0 98.7 jit_solution(9047395859559299107)
XLA Ops:
  0.0 97.7 %shard_map.82 = bf16[1,128,4096]{2,1,0:T(8,128)(2,1)S(1)} custom-call(bf16[1,128,4096]{2,1,0:T(8,128)(2,1)} %tok.1, bf16[1,4096,896]{2,1,0:T(8,128)(2,1)} %w_gate.1, bf16[1,4096,896]{2,1,0:T(8,128)(2,1)} %w_up.1, bf16[1,896,4096]{2,1,0:T(8,128)(2,1)} %w_down.1, s32[1,4,512]{2,1,0:T(4,128)} %bitcast.3, s32[1,4,512]{2,1,0:T(4,128)} %bitcast.4, ...), custom_call_target="tpu_custom_call" | custom-call | tf_op jit(solution)/shard_map/pallas_call | solution.py:510
  97.7 1.0 copy.10
